TPU v7x, 128 devices: a whole 4x4x4 slice. The times are simulated.
128 devices in a mesh: row: 8 (over y, x_hi), col: 16 (over z, x_lo, core).
Axes of the slice: x: 4 (x_hi: 2, x_lo: 2; x = x_hi * 2 + x_lo), y: 4, z: 4, core: 2. Of those that a mesh axis runs over, the one named last changes fastest.
Arguments:
- model_gradient: float32 [3, 512, 512, 256], P(None, 'row', 'col'), may hold values from -6 to 6
- filter_x: float32 [512, 512], replicated, may hold values from 0 to 1, as said below
- filter_y: float32 [512, 512], replicated, may hold values from 0 to 1, as said below
- filter_z: float32 [256, 256], replicated, may hold values from 0 to 1, as said below
- depth_scale: float32 [3, 256], replicated, may hold values from 0.3 to 3
Outputs:
- smoothed: float32 [3, 512, 512, 256], P(None, 'row', 'col')
Inputs may be any that keep to these rules, and one draw needn't show every extreme that they name: `filter_x`: each row is a nonnegative smoothing kernel of its own width plus one half on the diagonal; rows sum to one. `filter_y`: each row is a nonnegative smoothing kernel of its own width plus one half on the diagonal; rows sum to one. `filter_z`: each row is a nonnegative smoothing kernel of its own width plus one half on the diagonal; rows sum to one.
All inputs are finite; a program needn't handle non-finite values.
Results may differ from a plain program's by a relative error of at most 0.0001.
Values sent between devices are 32-bit elements; how exact they have to be, the bound alone decides.
A program may use at most 128 MiB of HBM per device.

v0:
```python
import jax
import jax.numpy as jnp
from jax import lax
from jax.sharding import PartitionSpec as P


def plane_filter(incoming_part, filter_x, filter_y, rows, cols):
    highest_accuracy = lax.Precision.HIGHEST
    params, xloc, yloc = (incoming_part.shape[0], incoming_part.shape[1], incoming_part.shape[2])
    matrix_x = filter_x.reshape(rows, xloc, rows, xloc)
    lateral_y_matrix = filter_y.reshape(cols, yloc, cols, yloc)
    partial_value = jnp.einsum(
        "ABRa,pabRSz->ABpbSz", matrix_x, incoming_part, precision=highest_accuracy
    )
    return jnp.einsum(
        "CDSb,ABpbSz->ACpBDz", lateral_y_matrix, partial_value, precision=highest_accuracy
    )


def shards(model_gradient, filter_x, filter_y, filter_z, depth_scale):
    highest_accuracy = lax.Precision.HIGHEST
    rows = lax.axis_size("row")
    cols = lax.axis_size("col")
    params, xloc, yloc, depth = model_gradient.shape
    scaled_filter = depth_scale[:, :, None] * filter_z[None, :, :]
    column_first = jnp.einsum(
        "pkz,pabz->pabk", scaled_filter, model_gradient, precision=highest_accuracy
    )
    depth_block = depth // (rows * cols)
    outgoing = column_first.reshape(params, xloc, yloc, rows * cols, depth_block)
    incoming_part = lax.all_to_all(
        outgoing, ("row", "col"), split_axis=3, concat_axis=3, tiled=True
    )
    incoming_part = incoming_part.reshape(params, xloc, yloc, rows, cols, depth_block)
    planes = plane_filter(incoming_part, filter_x, filter_y, rows, cols)
    planes = planes.reshape(rows * cols, params, xloc, yloc, depth_block)
    result = lax.all_to_all(planes, ("row", "col"), split_axis=0, concat_axis=4, tiled=True)
    return result.reshape(params, xloc, yloc, depth)


def solution(mesh):
    return jax.shard_map(
        shards,
        mesh=mesh,
        in_specs=(P(None, "row", "col", None), P(), P(), P(), P()),
        out_specs=P(None, "row", "col", None),
        check_vma=False,
    )
```

profile of v0, /device:TPU:1, one launch (start us, length us, event | category | flops | bytes accessed | tf_op | source)
XLA Modules:
  0.0 431.2 jit_solution(3917413412582936384)
XLA Ops:
  0.0 13.3 %fusion.11 = f32[3,64,32,256]{3,1,2,0:T(8,128)} fusion(f32[3,64,32,256]{3,2,1,0:T(8,128)} %param.5, f32[256,256]{1,0:T(8,128)} %param.8, f32[3,256]{1,0:T(4,128)} %param.9), kind=kOutput, calls=%fused_computation.9 | convolution fusion | flops 4832034816 | bytes 12848128 | tf_op jit(solution)/shard_map/pkz,pabz->pabk/dot_general | solution.py:26
  13.3 12.6 %copy.23 = f32[3,64,32,256]{1,2,3,0:T(8,128)} copy(f32[3,64,32,256]{3,1,2,0:T(8,128)} %fusion.11) | data formatting | bytes 12582912 | tf_op jit(solution)/shard_map/pkz,pabz->pabk/dot_general | solution.py:26
  25.9 12.0 %copy.57 = f32[3,64,32,128,2]{1,2,4,0,3:T(8,128)} copy(f32[3,64,32,128,2]{1,2,4,3,0:T(8,128)} %bitcast.44) | data formatting | bytes 12582912 | tf_op jit(solution)/shard_map/reshape | solution.py:30
  38.0 13.2 %reshape.34 = f32[128,1,12288]{2,1,0:T(1,128)} reshape(f32[128,3,2,32,64]{4,3,2,1,0:T(8,128)} %bitcast.45) | data formatting | bytes 12582912
  51.1 0.0 copy-start.1
  51.1 23.1 %all-to-all-start = ((f32[128,1,12288]{2,1,0:T(1,128)}), f32[128,1,12288]{2,1,0:T(1,128)}, u32[]{:S(2)}, u32[]{:S(2)}) async-start(f32[128,1,12288]{2,1,0:T(1,128)} %reshape.34), calls=%async_computation | async-start | bytes 12582912 | tf_op jit(solution)/shard_map/all_to_all | solution.py:31
  74.3 0.0 copy-done.1
  74.3 0.4 reshape.23
  74.7 3.8 reshape.24
  78.5 72.7 %all-to-all-done = f32[128,1,12288]{2,1,0:T(1,128)} async-done(((f32[128,1,12288]{2,1,0:T(1,128)}), f32[128,1,12288]{2,1,0:T(1,128)}, u32[]{:S(2)}, u32[]{:S(2)}) %all-to-all-start) | async-done | bytes 6291488 | tf_op jit(solution)/shard_map/all_to_all | solution.py:31
  151.3 0.5 broadcast.2
  151.8 19.4 %reduce = f32[128,12288]{1,0:T(8,128)} reduce(f32[128,1,12288]{2,1,0:T(1,128)} %all-to-all-done, f32[]{:T(128)} %broadcast.2), dimensions={1}, to_apply=%all_to_all.14.reduce_sub_computation | reduce | bytes 12582916 | tf_op jit(solution)/shard_map/all_to_all | solution.py:31
  171.2 10.8 %reshape.35 = f32[128,3,2,32,64]{4,3,2,1,0:T(8,128)} reshape(f32[128,12288]{1,0:T(8,128)} %reduce) | data formatting | bytes 12582912
  182.0 0.0 copy-start
  182.0 43.6 %fusion.2 = f32[3,32,16,2,8,64,1]{5,1,6,2,3,0,4:T(8,128)S(1)} fusion(f32[3,64,32,8,16,2]{1,2,5,0,4,3:T(8,128)} %bitcast.48, f32[8,64,8,64,1,1,1]{3,2,1,0,6,5,4:T(8,128)S(1)} %bitcast.50), kind=kOutput, calls=%fused_computation.2 | convolution fusion | flops 9663676416 | bytes 13631488 | tf_op jit(solution)/shard_map/ABRa,pabRSz->ABpbSz/dot_general | solution.py:12
  225.6 0.0 copy-done
  225.6 28.0 %fusion.7 = f32[8,16,3,64,32,2]{3,4,1,5,2,0:T(8,128)} fusion(f32[3,32,16,2,8,64,1]{5,1,6,2,3,0,4:T(8,128)S(1)} %fusion.2, f32[16,32,16,32,1,1,1]{3,2,1,0,6,5,4:T(8,128)S(1)} %bitcast.49), kind=kOutput, calls=%fused_computation.7 | convolution fusion | flops 9663676416 | bytes 13631488 | tf_op jit(solution)/shard_map/CDSb,ABpbSz->ACpBDz/dot_general | solution.py:15
  253.6 11.3 %copy.29 = f32[8,16,3,64,32,2]{3,4,5,2,1,0:T(8,128)} copy(f32[8,16,3,64,32,2]{3,4,1,5,2,0:T(8,128)} %fusion.7) | data formatting | bytes 12582912 | tf_op jit(solution)/shard_map/CDSb,ABpbSz->ACpBDz/transpose | solution.py:15
  265.0 13.2 %reshape.36 = f32[128,1,12288]{2,1,0:T(1,128)} reshape(f32[128,3,2,32,64]{4,3,2,1,0:T(8,128)} %bitcast.46) | data formatting | bytes 12582912
  278.1 86.1 %all_to_all.20 = f32[128,1,12288]{2,1,0:T(1,128)} all-to-all(f32[128,1,12288]{2,1,0:T(1,128)} %reshape.36), channel_id=1, replica_groups=mesh['row'=8,'col'=16] {'row','col'}, dimensions={0} | all-to-all | bytes 12582912 | tf_op jit(solution)/shard_map/all_to_all | solution.py:37
  364.3 19.4 %reduce.1 = f32[128,12288]{1,0:T(8,128)} reduce(f32[128,1,12288]{2,1,0:T(1,128)} %all_to_all.20, f32[]{:T(128)} %broadcast.2), dimensions={1}, to_apply=%all_to_all.15.reduce_sub_computation | reduce | bytes 12582916 | tf_op jit(solution)/shard_map/all_to_all | solution.py:37
  383.7 10.8 %reshape.37 = f32[128,3,2,32,64]{4,3,2,1,0:T(8,128)} reshape(f32[128,12288]{1,0:T(8,128)} %reduce.1) | data formatting | bytes 12582912
  394.5 12.0 %bitcast_bitcast_fusion = f32[1,3,64,32,128,2]{2,3,5,1,4,0:T(8,128)} fusion(f32[128,3,2,32,64]{4,3,2,1,0:T(8,128)} %reshape.37), kind=kLoop, calls=%fused_computation.15 | loop fusion | bytes 12582912 | tf_op jit(solution)/shard_map/all_to_all | solution.py:37
  406.5 12.1 %copy.30 = f32[1,3,64,32,128,2]{2,3,5,4,1,0:T(8,128)} copy(f32[1,3,64,32,128,2]{2,3,5,1,4,0:T(8,128)} %bitcast_bitcast_fusion) | data formatting | bytes 12582912 | tf_op jit(solution)/shard_map/all_to_all | solution.py:37
  418.7 12.1 %copy.31 = f32[3,64,32,256]{3,2,1,0:T(8,128)} copy(f32[3,64,32,256]{1,2,3,0:T(8,128)} %bitcast.47) | data formatting | bytes 12582912 | tf_op jit(solution)/shard_map/reshape | solution.py:38
Async XLA Ops:
  51.1 23.1 %copy-start.1 = (f32[512,512]{1,0:T(8,128)S(1)}, f32[512,512]{1,0:T(8,128)}, u32[]{:S(2)}) copy-start(f32[512,512]{1,0:T(8,128)} %param.6) | copy-start | bytes 3145732
  51.1 100.1 %all-to-all-start = ((f32[128,1,12288]{2,1,0:T(1,128)}), f32[128,1,12288]{2,1,0:T(1,128)}, u32[]{:S(2)}, u32[]{:S(2)}) async-start(f32[128,1,12288]{2,1,0:T(1,128)} %reshape.34), calls=%async_computation | async-start | bytes 12582912 | tf_op jit(solution)/shard_map/all_to_all | solution.py:31
  182.0 43.6 %copy-start = (f32[16,32,16,32]{3,2,1,0:T(8,128)S(1)}, f32[16,32,16,32]{3,2,1,0:T(8,128)}, u32[]{:S(2)}) copy-start(f32[16,32,16,32]{3,2,1,0:T(8,128)} %reshape.24) | copy-start | bytes 3145732
where the time goes:
time: 434 us; the launch traced here: 431 us
  local copies, waits for them, and re-layouts  125 us (29%)
  blocking collectives  86.1 us (20%)
  matrix products  84.9 us (20%)
  waiting for transfers between devices  72.7 us (17%)
  other arithmetic  38.8 us (9%)
  starting transfers between devices  23.1 us (5%)
    all_to_all x1, blocking collectives, shards(): lax.all_to_all(planes, ('row', 'col'), split_axis=0, concat_axis=4, tiled...  86.1 us
    all_to_all x1, waiting for transfers between devices, shards(): lax.all_to_all(outgoing, ('row', 'col'), split_axis=3, concat_axis=3, til...  72.7 us
    unnamed x8, local copies, waits for them, and re-layouts  48 us
    dot_general x1, matrix products, plane_filter(): jnp.einsum('ABRa,pabRSz->ABpbSz', matrix_x, incoming_part, precision=high...  43.6 us
    dot_general x1, matrix products, plane_filter(): jnp.einsum('CDSb,ABpbSz->ACpBDz', lateral_y_matrix, partial_value, precis...  28 us
    all_to_all x2, local copies, waits for them, and re-layouts, shards(): lax.all_to_all(planes, ('row', 'col'), split_axis=0, concat_axis=4, tiled...  24.2 us
    all_to_all x1, starting transfers between devices, shards(): lax.all_to_all(outgoing, ('row', 'col'), split_axis=3, concat_axis=3, til...  23.1 us
    all_to_all x1, other arithmetic, shards(): lax.all_to_all(planes, ('row', 'col'), split_axis=0, concat_axis=4, tiled...  19.4 us
  transfers between devices with their start and end apart: 1, of which 1 were waited for; matrix products, arithmetic and copies ran while one was open for 1% of the time, Pallas kernels for 0%

commit v1 on v0

v1 whole, which is shorter than its diff:
```python
import jax
import jax.numpy as jnp
from jax import lax
from jax.experimental import pallas as pl
from jax.experimental.pallas import tpu as pltpu
from jax.sharding import PartitionSpec as P

MESH = pl.DeviceIdType.MESH
F32, BF16 = jnp.float32, jnp.bfloat16
ORDER = ("xyz", "yzx", "zxy")
CHUNKS = [(half, p) for half in range(2) for p in range(3)]


def split(value):
    high = value.astype(BF16)
    return high, (value - high.astype(F32)).astype(BF16)


def swap_blocks(parts):
    lane = lax.broadcasted_iota(jnp.int32, parts[0].shape, 1)
    low64, low32 = lane < 64, lane % 64 < 32
    mid = [None] * 4
    for e in range(2):
        one, two = parts[e], parts[e + 2]
        mid[e] = jnp.where(low64, one, pltpu.roll(two, 64, 1))
        mid[e + 2] = jnp.where(low64, pltpu.roll(one, 64, 1), two)
    out = [None] * 4
    for e in (0, 2):
        one, two = mid[e], mid[e + 1]
        out[e] = jnp.where(low32, one, pltpu.roll(two, 32, 1))
        out[e + 1] = jnp.where(low32, pltpu.roll(one, 96, 1), two)
    return out


def dot3(a_high, a_low, b_high, b_low):
    def dot(a, b):
        return jnp.dot(a, b, preferred_element_type=F32)

    return dot(a_high, b_high) + dot(a_low, b_high) + dot(a_high, b_low)


def kernel(
    g_hbm, fx_hbm, fy_hbm, fz_hbm, scale_ref, out_hbm,
    s0, r1, r2, r3, b1, b2, b3,
    wbuf, fxh, fxl, fyh, fyl, fzh, fzl, ph, pll, qh, ql, obuf,
    send_sem, recv_sem, in_sem, w_sem, out_sem,
):
    row, col = lax.axis_index("row"), lax.axis_index("col")
    me = {"x": (row % 2) * 2 + (col // 2) % 2, "y": row // 2, "z": col // 4}
    core = col % 2

    def device(at, k):
        x = at["x"]
        return (at["y"] * 2 + x // 2, at["z"] * 4 + (x % 2) * 2 + k)

    def along(dim, step, flip):
        at = dict(me)
        at[dim] = (me[dim] + step) % 4
        return at, (core + flip) % 2

    barrier = pltpu.get_barrier_semaphore()
    partners = [along(d, s, f) for d in "xyz" for s in (1, 2, 3) for f in (0, 1)]
    partners.append(along("x", 0, 1))
    for at, k in partners:
        pl.semaphore_signal(barrier, inc=1, device_id=device(at, k), device_id_type=MESH)

    def load_in(p, j):
        c = j * 3 + p
        return pltpu.make_async_copy(
            g_hbm.at[p, :, pl.ds(j * 128, 128)], b3.at[c], in_sem.at[c]
        )

    fz_copy = pltpu.make_async_copy(fz_hbm, wbuf.at[2, pl.ds(0, 256), pl.ds(0, 256)], w_sem.at[2])
    fz_copy.start()
    for p in range(3):
        for j in range(2):
            load_in(p, j).start()
    fx_copy = pltpu.make_async_copy(fx_hbm, wbuf.at[0], w_sem.at[0])
    fy_copy = pltpu.make_async_copy(fy_hbm, wbuf.at[1], w_sem.at[1])
    fx_copy.start()
    fy_copy.start()

    def transfers(c, stage):
        order = ORDER[c % 3]
        dim = order[(0, 1, 2, 2, 1, 0)[stage]]
        mine = me[dim]
        found = []
        for step in (1, 3, 2, 0):
            for flip in (0, 1) if stage in (0, 5) else (0,):
                if step == 0 and flip == 0:
                    continue
                at, k = along(dim, step, flip)
                d = at[dim]
                slot, own = d * 2 + k, mine * 2 + core
                if stage == 0:
                    src, dst = s0.at[c, pl.ds(slot * 256, 256)], r1.at[c, own]
                elif stage == 1:
                    src, dst = r1.at[c, :, pl.ds(d * 64, 64)], r2.at[c, :, mine]
                elif stage == 2:
                    src, dst = r2.at[c, :, :, pl.ds(d * 16, 16)], r3.at[c, :, :, mine]
                elif stage == 3:
                    src, dst = r3.at[c, :, :, d], b1.at[c, :, :, pl.ds(mine * 16, 16)]
                elif stage == 4:
                    src, dst = b1.at[c, :, d], b2.at[c, :, pl.ds(mine * 64, 64)]
                else:
                    src, dst = b2.at[c, slot], b3.at[c, pl.ds(own * 256, 256)]
                found.append(
                    pltpu.make_async_remote_copy(
                        src, dst, send_sem.at[c, stage], recv_sem.at[c, stage],
                        device_id=device(at, k), device_id_type=MESH,
                    )
                )
        return found

    def send(c, stage):
        for copy in transfers(c, stage):
            copy.start()
        keep(c, stage)

    def keep(c, stage):
        mine = me[ORDER[c % 3][(0, 1, 2, 2, 1, 0)[stage]]]
        own = mine * 2 + core
        if stage == 0:
            r1[c, own] = s0[c, pl.ds(pl.multiple_of(own * 256, 256), 256)]
        elif stage == 5:
            b3[c, pl.ds(pl.multiple_of(own * 256, 256), 256)] = b2[c, own]
        else:

            @pl.loop(0, 8)
            def _(i):
                if stage == 1:
                    r2[c, i, mine] = r1[c, i, pl.ds(pl.multiple_of(mine * 64, 64), 64)]
                elif stage == 2:
                    for k in range(4):
                        r3[c, i, k, mine] = r2[c, i, k, pl.ds(pl.multiple_of(mine * 16, 16), 16)]
                elif stage == 3:
                    for k in range(4):
                        b1[c, i, k, pl.ds(pl.multiple_of(mine * 16, 16), 16)] = r3[c, i, k, mine]
                else:
                    b2[c, i, pl.ds(pl.multiple_of(mine * 64, 64), 64)] = b1[c, i, mine]

    def arrived(c, stage):
        ref = (
            r1.at[c, pl.ds(0, 7)], r2.at[c, pl.ds(0, 6)], r3.at[c, pl.ds(0, 6)],
            b1.at[c, pl.ds(0, 6)], b2.at[c, pl.ds(0, 6)], b3.at[c, pl.ds(0, 7 * 256)],
        )[stage]
        pltpu.make_async_copy(ref, ref, recv_sem.at[c, stage]).wait()

    def sent(c, stage):
        ref = (
            r1.at[c, pl.ds(0, 7)], r2.at[c, pl.ds(0, 6)], r3.at[c, pl.ds(0, 6)],
            b1.at[c, pl.ds(0, 6)], b2.at[c, pl.ds(0, 6)], b3.at[c, pl.ds(0, 7 * 256)],
        )[stage]
        pltpu.make_async_copy(ref, ref, send_sem.at[c, stage]).wait()

    fz_copy.wait()
    fzh[...], fzl[...] = split(wbuf[2, 0:256, 0:256])

    def depth(p):
        for j in range(2):
            load_in(p, j).wait()

        @pl.loop(0, 8)
        def _(it):
            rows = []
            for u in range(2):
                for b in range(4):
                    at = pl.multiple_of((b * 16 + it * 2 + u) * 32, 32)
                    rows.append(
                        jnp.concatenate([b3[p, pl.ds(at, 32)], b3[3 + p, pl.ds(at, 32)]], axis=1)
                    )
            high, low = split(jnp.concatenate(rows, axis=0))

            def dot(a, b):
                return lax.dot_general(
                    a, b, (((1,), (1,)), ((), ())), preferred_element_type=F32
                )

            for j in range(2):
                fh, fl = fzh[pl.ds(j * 128, 128)], fzl[pl.ds(j * 128, 128)]
                got = dot(fh, high) + dot(fl, high) + dot(fh, low)
                for u in range(2):
                    s0[j * 3 + p, pl.ds(it * 2 + u, 128, stride=16)] = got[:, u * 128 : u * 128 + 128]

    depth(0)
    pl.semaphore_wait(barrier, len(partners))
    send(0, 0)
    depth(1)
    send(1, 0)
    depth(2)
    send(2, 0)
    for c in (3, 4, 5):
        send(c, 0)

    fx_copy.wait()
    fy_copy.wait()

    @pl.loop(0, 4)
    def _(i):
        at = pl.ds(pl.multiple_of(i * 128, 128), 128)
        fxh[at], fxl[at] = split(wbuf[0, at])
        turned = jnp.concatenate([wbuf[1, pl.ds(k * 128, 128), at].T for k in range(4)], axis=1)
        fyh[at], fyl[at] = split(turned)

    def units(c, r, q):
        found = []
        for e in range(4):
            at = {"x": (r % 2) * 2 + e // 2, "y": r // 2, "z": q}
            one, two, three = (at[d] for d in ORDER[c % 3])
            found.append((one * 2 + e % 2, two, three))
        return found

    def smooth(c):
        @pl.loop(0, 8)
        def _(r):
            for q in range(4):
                blocks = swap_blocks([r3[c, i, k, m] for i, k, m in units(c, r, q)])
                for b in range(4):
                    at = pl.ds(pl.multiple_of(r * 64 + b * 16, 16), 16)
                    high, low = split(blocks[b])
                    ph[at, q * 128 : q * 128 + 128] = high
                    pll[at, q * 128 : q * 128 + 128] = low

        @pl.loop(0, 2)
        def _(ib):
            at = pl.ds(pl.multiple_of(ib * 256, 256), 256)
            for n in range(2):
                cut = slice(n * 256, n * 256 + 256)
                qh[:, cut], ql[:, cut] = split(dot3(fxh[at], fxl[at], ph[:, cut], pll[:, cut]))
            for n in range(2):
                cut = slice(n * 256, n * 256 + 256)
                obuf[:, cut] = dot3(qh[...], ql[...], fyh[:, cut], fyl[:, cut])

            @pl.loop(0, 4)
            def _(rr):
                r = ib * 4 + rr
                for q in range(4):
                    blocks = swap_blocks(
                        [
                            obuf[pl.ds(pl.multiple_of(rr * 64 + b * 16, 16), 16), q * 128 : q * 128 + 128]
                            for b in range(4)
                        ]
                    )
                    for e, (i, k, m) in enumerate(units(c, r, q)):
                        r3[c, i, k, m] = blocks[e]

    for stage in (1, 2):
        for c in range(6):
            arrived(c, stage - 1)
            send(c, stage)
    for c in range(6):
        arrived(c, 2)
        smooth(c)
        send(c, 3)
    for stage in (4, 5):
        for c in range(6):
            arrived(c, stage - 1)
            send(c, stage)

    def store_out(c):
        half, p = CHUNKS[c]
        return pltpu.make_async_copy(
            r1.at[c], out_hbm.at[p, :, :, pl.ds(half * 128, 128)], out_sem.at[c]
        )

    for c in range(6):
        half, p = CHUNKS[c]
        sent(c, 1)
        arrived(c, 5)

        @pl.loop(0, 16)
        def _(m):
            turned = b3[c, pl.ds(m, 128, stride=16)].T
            turned = turned * scale_ref[p : p + 1, half * 128 : half * 128 + 128]
            for b in range(4):
                at = pl.multiple_of((m % 8) * 32, 32)
                r1[c, b * 2 + m // 8, pl.ds(at, 32)] = turned[b * 32 : b * 32 + 32]

        store_out(c).start()
    for c in range(6):
        for stage in (0, 2, 3, 4, 5):
            sent(c, stage)
        store_out(c).wait()


def shards(model_gradient, filter_x, filter_y, filter_z, depth_scale):
    params, xloc, yloc, depth = model_gradient.shape
    anywhere = pl.BlockSpec(memory_space=pl.ANY)
    result = pl.pallas_call(
        kernel,
        out_shape=jax.ShapeDtypeStruct((params, 8, 256, depth), F32),
        in_specs=[anywhere] * 4 + [pl.BlockSpec(memory_space=pltpu.VMEM)],
        out_specs=anywhere,
        scratch_shapes=[
            pltpu.VMEM((6, 2048, 128), F32),
            pltpu.VMEM((6, 8, 256, 128), F32),
            pltpu.VMEM((6, 8, 4, 64, 128), F32),
            pltpu.VMEM((6, 8, 4, 4, 16, 128), F32),
            pltpu.VMEM((6, 8, 4, 64, 128), F32),
            pltpu.VMEM((6, 8, 256, 128), F32),
            pltpu.VMEM((6, 2048, 128), F32),
            pltpu.VMEM((3, 512, 512), F32),
            pltpu.VMEM((512, 512), BF16),
            pltpu.VMEM((512, 512), BF16),
            pltpu.VMEM((512, 512), BF16),
            pltpu.VMEM((512, 512), BF16),
            pltpu.VMEM((256, 256), BF16),
            pltpu.VMEM((256, 256), BF16),
            pltpu.VMEM((512, 512), BF16),
            pltpu.VMEM((512, 512), BF16),
            pltpu.VMEM((256, 512), BF16),
            pltpu.VMEM((256, 512), BF16),
            pltpu.VMEM((256, 512), F32),
            pltpu.SemaphoreType.DMA((6, 6)),
            pltpu.SemaphoreType.DMA((6, 6)),
            pltpu.SemaphoreType.DMA((6,)),
            pltpu.SemaphoreType.DMA((3,)),
            pltpu.SemaphoreType.DMA((6,)),
        ],
        compiler_params=pltpu.CompilerParams(
            collective_id=0, has_side_effects=True, vmem_limit_bytes=60 * 2**20
        ),
        name="smooth_planes",
    )(model_gradient.reshape(params, xloc * yloc, depth), filter_x, filter_y, filter_z, depth_scale)
    return result.reshape(params, xloc, yloc, depth)


def solution(mesh):
    return jax.shard_map(
        shards,
        mesh=mesh,
        in_specs=(P(None, "row", "col", None), P(), P(), P(), P()),
        out_specs=P(None, "row", "col", None),
        check_vma=False,
    )
```

time: 434 us -> 177 us (0.41)
  Pallas kernels: 0 us -> 170 us
  local copies, waits for them, and re-layouts: 125 us -> 6.61 us
  blocking collectives: 86.1 us -> 0 us
  matrix products: 84.9 us -> 0 us
  waiting for transfers between devices: 72.7 us -> 0 us
  other arithmetic: 38.8 us -> 0 us
  starting transfers between devices: 23.1 us -> 0 us
    pallas_call x0 -> x1, Pallas kernels: none -> 170 us  [shards(): pl.pallas_call(kernel, out_shape=jax.ShapeDtypeStruct((params, 8, 256, de...]
    all_to_all x1 -> x0, blocking collectives: 86.1 us -> none  [shards(): lax.all_to_all(planes, ('row', 'col'), split_axis=0, concat_axis=4, tiled...]
    dot_general x3 -> x0, matrix products: 84.9 us -> none  [the longest x1 43.6 us: plane_filter(): jnp.einsum('ABRa,pabRSz->ABpbSz', matrix_x, incoming_part, precision=high...]
    all_to_all x1 -> x0, waiting for transfers between devices: 72.7 us -> none  [shards(): lax.all_to_all(outgoing, ('row', 'col'), split_axis=3, concat_axis=3, til...]
    unnamed x8 -> x1, local copies, waits for them, and re-layouts: 48 us -> 6.61 us
    all_to_all x2 -> x0, other arithmetic: 38.8 us -> none  [the longest x1 19.4 us: shards(): lax.all_to_all(planes, ('row', 'col'), split_axis=0, concat_axis=4, tiled...]
    reshape x4 -> x0, local copies, waits for them, and re-layouts: 28.4 us -> none  [the longest x1 12.1 us: shards(): return result.reshape(params, xloc, yloc, depth)]
    all_to_all x3 -> x0, local copies, waits for them, and re-layouts: 24.7 us -> none  [the longest x2 24.2 us: shards(): lax.all_to_all(planes, ('row', 'col'), split_axis=0, concat_axis=4, tiled...]
  transfers between devices with their start and end apart: 1 -> 0, of which waited for: 1 -> 0; matrix products, arithmetic and copies ran while one was open for 1% -> 0% of each run, Pallas kernels for 0% -> 0%
where the time goes in v1:
time: 177 us
  Pallas kernels  170 us (96%)
  local copies, waits for them, and re-layouts  6.61 us (4%)
    pallas_call x1, Pallas kernels, shards(): pl.pallas_call(kernel, out_shape=jax.ShapeDtypeStruct((params, 8, 256, de...  170 us
    unnamed x1, local copies, waits for them, and re-layouts  6.61 us

profile of v1, /device:TPU:1, one launch (start us, length us, event | category | flops | bytes accessed | tf_op | source)
XLA Modules:
  0.0 177.1 jit_solution(2870461586563439170)
XLA Ops:
  0.0 170.4 %smooth_planes.1 = f32[3,8,256,256]{3,2,1,0:T(8,128)} custom-call(f32[3,2048,256]{2,1,0:T(8,128)} %bitcast.3, f32[512,512]{1,0:T(8,128)} %fx_hbm.1, f32[512,512]{1,0:T(8,128)} %fy_hbm.1, f32[256,256]{1,0:T(8,128)} %fz_hbm.1, f32[3,256]{1,0:T(4,128)} %scale_ref.1), custom_call_target="tpu_custom_call" | custom-call | tf_op jit(solution)/shard_map/smooth_planes/pallas_call | solution.py:289
  170.4 6.6 %copy.7 = f32[3,64,32,256]{3,2,1,0:T(8,128)} copy(f32[3,64,32,256]{3,2,1,0:T(8,128)} %bitcast.2) | data formatting | bytes 12582912

commit v2 on v1

--- a/solution.py
+++ b/solution.py
@@ -40,10 +40,10 @@
 
 
 def kernel(
-    g_hbm, fx_hbm, fy_hbm, fz_hbm, scale_ref, out_hbm,
+    g_hbm, fx_hbm, fy_hbm, fz_hbm, scale_ref, out,
     s0, r1, r2, r3, b1, b2, b3,
     wbuf, fxh, fxl, fyh, fyl, fzh, fzl, ph, pll, qh, ql, obuf,
-    send_sem, recv_sem, in_sem, w_sem, out_sem,
+    send_sem, recv_sem, in_sem, w_sem,
 ):
     row, col = lax.axis_index("row"), lax.axis_index("col")
     me = {"x": (row % 2) * 2 + (col // 2) % 2, "y": row // 2, "z": col // 4}
@@ -113,9 +113,11 @@
         return found
 
     def send(c, stage):
-        for copy in transfers(c, stage):
-            copy.start()
-        keep(c, stage)
+        with jax.named_scope(f"send#c={c}#s={stage}"):
+            for copy in transfers(c, stage):
+                copy.start()
+        with jax.named_scope(f"keep#c={c}#s={stage}"):
+            keep(c, stage)
 
     def keep(c, stage):
         mine = me[ORDER[c % 3][(0, 1, 2, 2, 1, 0)[stage]]]
@@ -144,7 +146,8 @@
             r1.at[c, pl.ds(0, 7)], r2.at[c, pl.ds(0, 6)], r3.at[c, pl.ds(0, 6)],
             b1.at[c, pl.ds(0, 6)], b2.at[c, pl.ds(0, 6)], b3.at[c, pl.ds(0, 7 * 256)],
         )[stage]
-        pltpu.make_async_copy(ref, ref, recv_sem.at[c, stage]).wait()
+        with jax.named_scope(f"arrive#c={c}#s={stage}"):
+            pltpu.make_async_copy(ref, ref, recv_sem.at[c, stage]).wait()
 
     def sent(c, stage):
         ref = (
@@ -156,11 +159,10 @@
     fz_copy.wait()
     fzh[...], fzl[...] = split(wbuf[2, 0:256, 0:256])
 
-    def depth(p):
-        for j in range(2):
-            load_in(p, j).wait()
-
-        @pl.loop(0, 8)
+    def depth(p, j):
+        fh, fl = fzh[j * 128 : j * 128 + 128], fzl[j * 128 : j * 128 + 128]
+
+        @pl.loop(0, 8, unroll=4)
         def _(it):
             rows = []
             for u in range(2):
@@ -176,31 +178,31 @@
                     a, b, (((1,), (1,)), ((), ())), preferred_element_type=F32
                 )
 
+            got = dot(fh, high) + dot(fl, high) + dot(fh, low)
+            for u in range(2):
+                s0[j * 3 + p, pl.ds(it * 2 + u, 128, stride=16)] = got[:, u * 128 : u * 128 + 128]
+
+    for c in range(6):
+        half, p = CHUNKS[c]
+        if half == 0:
             for j in range(2):
-                fh, fl = fzh[pl.ds(j * 128, 128)], fzl[pl.ds(j * 128, 128)]
-                got = dot(fh, high) + dot(fl, high) + dot(fh, low)
-                for u in range(2):
-                    s0[j * 3 + p, pl.ds(it * 2 + u, 128, stride=16)] = got[:, u * 128 : u * 128 + 128]
-
-    depth(0)
-    pl.semaphore_wait(barrier, len(partners))
-    send(0, 0)
-    depth(1)
-    send(1, 0)
-    depth(2)
-    send(2, 0)
-    for c in (3, 4, 5):
+                load_in(p, j).wait()
+        with jax.named_scope(f"depth#c={c}"):
+            depth(p, half)
+        if c == 0:
+            pl.semaphore_wait(barrier, len(partners))
         send(c, 0)
 
-    fx_copy.wait()
-    fy_copy.wait()
-
-    @pl.loop(0, 4)
-    def _(i):
-        at = pl.ds(pl.multiple_of(i * 128, 128), 128)
-        fxh[at], fxl[at] = split(wbuf[0, at])
-        turned = jnp.concatenate([wbuf[1, pl.ds(k * 128, 128), at].T for k in range(4)], axis=1)
-        fyh[at], fyl[at] = split(turned)
+    with jax.named_scope("weights"):
+        fx_copy.wait()
+        fy_copy.wait()
+
+        @pl.loop(0, 4)
+        def _(i):
+            at = pl.ds(pl.multiple_of(i * 128, 128), 128)
+            fxh[at], fxl[at] = split(wbuf[0, at])
+            turned = jnp.concatenate([wbuf[1, pl.ds(k * 128, 128), at].T for k in range(4)], axis=1)
+            fyh[at], fyl[at] = split(turned)
 
     def units(c, r, q):
         found = []
@@ -211,7 +213,7 @@
         return found
 
     def smooth(c):
-        @pl.loop(0, 8)
+        @pl.loop(0, 8, unroll=2)
         def _(r):
             for q in range(4):
                 blocks = swap_blocks([r3[c, i, k, m] for i, k, m in units(c, r, q)])
@@ -231,7 +233,7 @@
                 cut = slice(n * 256, n * 256 + 256)
                 obuf[:, cut] = dot3(qh[...], ql[...], fyh[:, cut], fyl[:, cut])
 
-            @pl.loop(0, 4)
+            @pl.loop(0, 4, unroll=2)
             def _(rr):
                 r = ib * 4 + rr
                 for q in range(4):
@@ -250,37 +252,33 @@
             send(c, stage)
     for c in range(6):
         arrived(c, 2)
-        smooth(c)
+        with jax.named_scope(f"smooth#c={c}"):
+            smooth(c)
         send(c, 3)
     for stage in (4, 5):
         for c in range(6):
             arrived(c, stage - 1)
             send(c, stage)
 
-    def store_out(c):
-        half, p = CHUNKS[c]
-        return pltpu.make_async_copy(
-            r1.at[c], out_hbm.at[p, :, :, pl.ds(half * 128, 128)], out_sem.at[c]
-        )
-
     for c in range(6):
         half, p = CHUNKS[c]
-        sent(c, 1)
         arrived(c, 5)
 
-        @pl.loop(0, 16)
-        def _(m):
-            turned = b3[c, pl.ds(m, 128, stride=16)].T
-            turned = turned * scale_ref[p : p + 1, half * 128 : half * 128 + 128]
-            for b in range(4):
-                at = pl.multiple_of((m % 8) * 32, 32)
-                r1[c, b * 2 + m // 8, pl.ds(at, 32)] = turned[b * 32 : b * 32 + 32]
-
-        store_out(c).start()
-    for c in range(6):
-        for stage in (0, 2, 3, 4, 5):
-            sent(c, stage)
-        store_out(c).wait()
+        with jax.named_scope(f"final#c={c}"):
+
+            @pl.loop(0, 16, unroll=4)
+            def _(m):
+                turned = b3[c, pl.ds(m, 128, stride=16)].T
+                turned = turned * scale_ref[p : p + 1, half * 128 : half * 128 + 128]
+                for b in range(4):
+                    at = pl.multiple_of((m % 8) * 32, 32)
+                    out[p, b * 2 + m // 8, pl.ds(at, 32), half * 128 : half * 128 + 128] = turned[
+                        b * 32 : b * 32 + 32
+                    ]
+    with jax.named_scope("drain"):
+        for c in range(6):
+            for stage in range(6):
+                sent(c, stage)
 
 
 def shards(model_gradient, filter_x, filter_y, filter_z, depth_scale):
@@ -288,9 +286,9 @@
     anywhere = pl.BlockSpec(memory_space=pl.ANY)
     result = pl.pallas_call(
         kernel,
-        out_shape=jax.ShapeDtypeStruct((params, 8, 256, depth), F32),
+        out_shape=pltpu.VMEM((params, 8, 256, depth), F32),
         in_specs=[anywhere] * 4 + [pl.BlockSpec(memory_space=pltpu.VMEM)],
-        out_specs=anywhere,
+        out_specs=pl.BlockSpec(memory_space=pltpu.VMEM),
         scratch_shapes=[
             pltpu.VMEM((6, 2048, 128), F32),
             pltpu.VMEM((6, 8, 256, 128), F32),
@@ -315,10 +313,9 @@
             pltpu.SemaphoreType.DMA((6, 6)),
             pltpu.SemaphoreType.DMA((6,)),
             pltpu.SemaphoreType.DMA((3,)),
-            pltpu.SemaphoreType.DMA((6,)),
         ],
         compiler_params=pltpu.CompilerParams(
-            collective_id=0, has_side_effects=True, vmem_limit_bytes=60 * 2**20
+            collective_id=0, has_side_effects=True, vmem_limit_bytes=53 * 2**20
         ),
         name="smooth_planes",
     )(model_gradient.reshape(params, xloc * yloc, depth), filter_x, filter_y, filter_z, depth_scale)

time: 177 us -> 159 us (0.90)
  Pallas kernels: 170 us -> 156 us
  local copies, waits for them, and re-layouts: 6.61 us -> 2.71 us
    pallas_call x1, Pallas kernels: 170 us -> 156 us  [shards(): pl.pallas_call(kernel, out_shape=pltpu.VMEM((params, 8, 256, depth), F32)...]
    unnamed x1, local copies, waits for them, and re-layouts: 6.61 us -> 2.71 us
where the time goes in v2:
time: 159 us
  Pallas kernels  156 us (98%)
  local copies, waits for them, and re-layouts  2.71 us (2%)
    pallas_call x1, Pallas kernels, shards(): pl.pallas_call(kernel, out_shape=pltpu.VMEM((params, 8, 256, depth), F32)...  156 us

profile of v2, /device:TPU:1, one launch (start us, length us, event | category | flops | bytes accessed | tf_op | source)
XLA Modules:
  0.0 159.0 jit_solution(4169542009663695434)
XLA Ops:
  0.0 156.3 %smooth_planes.1 = f32[3,8,256,256]{3,2,1,0:T(8,128)S(1)} custom-call(f32[3,2048,256]{2,1,0:T(8,128)} %bitcast.3, f32[512,512]{1,0:T(8,128)} %fx_hbm.1, f32[512,512]{1,0:T(8,128)} %fy_hbm.1, f32[256,256]{1,0:T(8,128)} %fz_hbm.1, f32[3,256]{1,0:T(4,128)} %scale_ref.1), custom_call_target="tpu_custom_call" | custom-call | tf_op jit(solution)/shard_map/smooth_planes/pallas_call | solution.py:287
  156.3 2.7 %copy.7 = f32[3,64,32,256]{3,2,1,0:T(8,128)} copy(f32[3,64,32,256]{3,2,1,0:T(8,128)S(1)} %bitcast.2) | data formatting | bytes 12582912

commit v3 on v2

v3 whole, which is shorter than its diff:
```python
import jax
import jax.numpy as jnp
from jax import lax
from jax.experimental import pallas as pl
from jax.experimental.pallas import tpu as pltpu
from jax.sharding import PartitionSpec as P

MESH = pl.DeviceIdType.MESH
F32, BF16 = jnp.float32, jnp.bfloat16
ORDER = ("xyz", "yzx", "zxy")
CHUNKS = [(half, p) for half in range(2) for p in range(3)]


def split(value):
    high = value.astype(BF16)
    return high, (value - high.astype(F32)).astype(BF16)


def swap_blocks(parts):
    lane = lax.broadcasted_iota(jnp.int32, parts[0].shape, 1)
    low64, low32 = lane < 64, lane % 64 < 32
    mid = [None] * 4
    for e in range(2):
        one, two = parts[e], parts[e + 2]
        mid[e] = jnp.where(low64, one, pltpu.roll(two, 64, 1))
        mid[e + 2] = jnp.where(low64, pltpu.roll(one, 64, 1), two)
    out = [None] * 4
    for e in (0, 2):
        one, two = mid[e], mid[e + 1]
        out[e] = jnp.where(low32, one, pltpu.roll(two, 32, 1))
        out[e + 1] = jnp.where(low32, pltpu.roll(one, 96, 1), two)
    return out


def dot3(a_high, a_low, b_high, b_low):
    def dot(a, b):
        return jnp.dot(a, b, preferred_element_type=F32)

    return dot(a_high, b_high) + dot(a_low, b_high) + dot(a_high, b_low)


def kernel(
    g_hbm, fx_hbm, fy_hbm, fz_hbm, scale_ref, out,
    s0, r1, r2, r3, b1, b2, b3,
    wbuf, fxh, fxl, fyh, fyl, fzh, fzl, ph, pll, qh, ql, pbuf,
    send_sem, recv_sem, in_sem, w_sem,
):
    row, col = lax.axis_index("row"), lax.axis_index("col")
    me = {"x": (row % 2) * 2 + (col // 2) % 2, "y": row // 2, "z": col // 4}
    core = col % 2

    def device(at, k):
        x = at["x"]
        return (at["y"] * 2 + x // 2, at["z"] * 4 + (x % 2) * 2 + k)

    def along(dim, step, flip):
        at = dict(me)
        at[dim] = (me[dim] + step) % 4
        return at, (core + flip) % 2

    def load_in(p, h):
        return pltpu.make_async_copy(g_hbm.at[p, :, h], out.at[p, :, h], in_sem.at[p, h])

    fz_copy = pltpu.make_async_copy(fz_hbm, wbuf.at[2, pl.ds(0, 256), pl.ds(0, 256)], w_sem.at[2])
    fx_copy = pltpu.make_async_copy(fx_hbm, wbuf.at[0], w_sem.at[0])
    fy_copy = pltpu.make_async_copy(fy_hbm, wbuf.at[1], w_sem.at[1])
    load_in(0, 0).start()
    fz_copy.start()
    load_in(1, 0).start()
    load_in(2, 0).start()

    barrier = pltpu.get_barrier_semaphore()
    partners = [along(d, s, f) for d in "xyz" for s in (1, 2, 3) for f in (0, 1)]
    partners.append(along("x", 0, 1))
    for at, k in partners:
        pl.semaphore_signal(barrier, inc=1, device_id=device(at, k), device_id_type=MESH)

    def transfers(c, stage, halves):
        order = ORDER[c % 3]
        dim = order[(0, 1, 2, 2, 1, 0)[stage]]
        mine = me[dim]
        found = []
        for step in (1, 3, 2, 0):
            for flip in (0, 1) if stage in (0, 5) else (0,):
                if step == 0 and flip == 0:
                    continue
                at, k = along(dim, step, flip)
                d = at[dim]
                slot, own = d * 2 + k, mine * 2 + core
                if stage == 0:
                    pairs = [
                        (s0.at[c, h, pl.ds(slot * 128, 128)], r1.at[c, h * 8 + own]) for h in halves
                    ]
                elif stage == 1:
                    pairs = [(r1.at[c, :, pl.ds(d * 32, 32)], r2.at[c, :, mine])]
                elif stage == 2:
                    pairs = [(r2.at[c, :, :, pl.ds(d * 8, 8)], r3.at[c, :, :, mine])]
                elif stage == 3:
                    pairs = [(r3.at[c, :, :, d], b1.at[c, :, :, pl.ds(mine * 8, 8)])]
                elif stage == 4:
                    pairs = [(b1.at[c, :, d], b2.at[c, :, pl.ds(mine * 32, 32)])]
                else:
                    pairs = [
                        (b2.at[c, h * 8 + slot], b3.at[c, h, pl.ds(own * 128, 128)]) for h in halves
                    ]
                for src, dst in pairs:
                    found.append(
                        pltpu.make_async_remote_copy(
                            src, dst, send_sem.at[c, stage], recv_sem.at[c, stage],
                            device_id=device(at, k), device_id_type=MESH,
                        )
                    )
        return found

    def send(c, stage, halves=(0, 1)):
        with jax.named_scope(f"send#c={c}#s={stage}"):
            for copy in transfers(c, stage, halves):
                copy.start()
        with jax.named_scope(f"keep#c={c}#s={stage}"):
            keep(c, stage, halves)

    def keep(c, stage, halves):
        mine = me[ORDER[c % 3][(0, 1, 2, 2, 1, 0)[stage]]]
        own = mine * 2 + core
        block = pl.ds(pl.multiple_of(own * 128, 128), 128)
        part = pl.ds(pl.multiple_of(mine * 32, 32), 32)
        unit = pl.ds(pl.multiple_of(mine * 8, 8), 8)
        if stage == 0:
            for h in halves:
                r1[c, h * 8 + own] = s0[c, h, block]
        elif stage == 5:
            for h in halves:
                b3[c, h, block] = b2[c, h * 8 + own]
        else:

            @pl.loop(0, 16, unroll=4)
            def _(i):
                if stage == 1:
                    r2[c, i, mine] = r1[c, i, part]
                elif stage == 2:
                    for k in range(4):
                        r3[c, i, k, mine] = r2[c, i, k, unit]
                elif stage == 3:
                    for k in range(4):
                        b1[c, i, k, unit] = r3[c, i, k, mine]
                else:
                    b2[c, i, part] = b1[c, i, mine]

    def whole(c, stage):
        if stage == 0:
            return r1.at[c, pl.ds(0, 14)]
        if stage == 5:
            return b2.at[c, pl.ds(0, 14)]
        return (r2, r3, b1, b2)[stage - 1].at[c, pl.ds(0, 12)]

    def arrived(c, stage):
        ref = whole(c, stage)
        with jax.named_scope(f"arrive#c={c}#s={stage}"):
            pltpu.make_async_copy(ref, ref, recv_sem.at[c, stage]).wait()

    def sent(c, stage):
        ref = whole(c, stage)
        pltpu.make_async_copy(ref, ref, send_sem.at[c, stage]).wait()

    fz_copy.wait()
    fzh[...], fzl[...] = split(wbuf[2, 0:256, 0:256])

    def depth(p, j, h):
        fh, fl = fzh[j * 128 : j * 128 + 128], fzl[j * 128 : j * 128 + 128]
        for it in range(4):
            rows = [
                out[p, b, h, m * 32 : m * 32 + 32] for m in (it * 2, it * 2 + 1) for b in range(4)
            ]
            high, low = split(jnp.concatenate(rows, axis=0))

            def dot(a, b):
                return lax.dot_general(
                    a, b, (((1,), (1,)), ((), ())), preferred_element_type=F32
                )

            got = dot(fh, high) + dot(fl, high) + dot(fh, low)
            for u in range(2):
                s0[j * 3 + p, h, pl.ds(it * 2 + u, 128, stride=8)] = got[:, u * 128 : u * 128 + 128]

    for h in range(2):
        for p in range(3):
            load_in(p, h).wait()
            if h == 0:
                load_in(p, 1).start()
            with jax.named_scope(f"depth#c={p}#h={h}"):
                depth(p, 0, h)
            if h == 0 and p == 2:
                fx_copy.start()
                fy_copy.start()
                with jax.named_scope("barrier"):
                    pl.semaphore_wait(barrier, len(partners))
                for c in range(3):
                    send(c, 0, (0,))
            if h == 1:
                send(p, 0, (1,))
    for c in (3, 4, 5):
        for h in range(2):
            with jax.named_scope(f"depth#c={c}#h={h}"):
                depth(c - 3, 1, h)
        send(c, 0)

    with jax.named_scope("weights"):
        fx_copy.wait()
        fy_copy.wait()

        @pl.loop(0, 4)
        def _(i):
            at = pl.ds(pl.multiple_of(i * 128, 128), 128)
            fxh[at], fxl[at] = split(wbuf[0, at])
            turned = jnp.concatenate([wbuf[1, pl.ds(k * 128, 128), at].T for k in range(4)], axis=1)
            fyh[at], fyl[at] = split(turned)

    def units(c, r, q):
        found = []
        for e in range(4):
            at = {"x": (r % 2) * 2 + e // 2, "y": r // 2, "z": q}
            one, two, three = (at[d] for d in ORDER[c % 3])
            found.append((one * 2 + e % 2, two, three))
        return found

    def smooth(c):
        def assemble(r, q):
            for h in range(2):
                blocks = swap_blocks([r3[c, h * 8 + i, k, m] for i, k, m in units(c, r, q)])
                for b in range(4):
                    at = slice(r * 64 + b * 16 + h * 8, r * 64 + b * 16 + h * 8 + 8)
                    pbuf[at, q * 128 : q * 128 + 128] = blocks[b]

        def scatter(r, q):
            for h in range(2):
                rows = [slice(r * 64 + b * 16 + h * 8, r * 64 + b * 16 + h * 8 + 8) for b in range(4)]
                blocks = swap_blocks([pbuf[at, q * 128 : q * 128 + 128] for at in rows])
                for e, (i, k, m) in enumerate(units(c, r, q)):
                    r3[c, h * 8 + i, k, m] = blocks[e]

        for q in range(4):
            for r in range(8):
                assemble(r, q)
            cut = slice(q * 128, q * 128 + 128)
            ph[:, cut], pll[:, cut] = split(pbuf[:, cut])
        for ib in range(2):
            at = slice(ib * 256, ib * 256 + 256)
            for n in range(2):
                cut = slice(n * 256, n * 256 + 256)
                qh[at, cut], ql[at, cut] = split(dot3(fxh[at], fxl[at], ph[:, cut], pll[:, cut]))
        for ib in range(2):
            at = slice(ib * 256, ib * 256 + 256)
            for n in range(2):
                cut = slice(n * 256, n * 256 + 256)
                pbuf[at, cut] = dot3(qh[at], ql[at], fyh[:, cut], fyl[:, cut])
            for r in range(ib * 4, ib * 4 + 4):
                for q in range(4):
                    scatter(r, q)

    for stage in (1, 2):
        for c in range(6):
            arrived(c, stage - 1)
            send(c, stage)
    order = (1, 2, 0, 4, 5, 3)
    for c in order:
        arrived(c, 2)
        with jax.named_scope(f"smooth#c={c}"):
            smooth(c)
        send(c, 3)
    for stage in (4, 5):
        for c in order:
            arrived(c, stage - 1)
            send(c, stage)

    for c in range(6):
        half, p = CHUNKS[c]
        arrived(c, 5)

        with jax.named_scope(f"final#c={c}"):

            for h in range(2):
                for m in range(8):
                    turned = b3[c, h, pl.ds(m, 128, stride=8)].T
                    turned = turned * scale_ref[p : p + 1, half * 128 : half * 128 + 128]
                    for b in range(4):
                        out[p, b, h, m * 32 : m * 32 + 32, half * 128 : half * 128 + 128] = turned[
                            b * 32 : b * 32 + 32
                        ]

    with jax.named_scope("drain"):
        for c in range(6):
            for stage in range(6):
                sent(c, stage)


def shards(model_gradient, filter_x, filter_y, filter_z, depth_scale):
    params, xloc, yloc, depth = model_gradient.shape
    anywhere = pl.BlockSpec(memory_space=pl.ANY)
    result = pl.pallas_call(
        kernel,
        out_shape=pltpu.VMEM((params, 4, 2, 256, depth), F32),
        in_specs=[anywhere] * 4 + [pl.BlockSpec(memory_space=pltpu.VMEM)],
        out_specs=pl.BlockSpec(memory_space=pltpu.VMEM),
        scratch_shapes=[
            pltpu.VMEM((6, 2, 1024, 128), F32),
            pltpu.VMEM((6, 16, 128, 128), F32),
            pltpu.VMEM((6, 16, 4, 32, 128), F32),
            pltpu.VMEM((6, 16, 4, 4, 8, 128), F32),
            pltpu.VMEM((6, 16, 4, 32, 128), F32),
            pltpu.VMEM((6, 16, 128, 128), F32),
            pltpu.VMEM((6, 2, 1024, 128), F32),
            pltpu.VMEM((3, 512, 512), F32),
            pltpu.VMEM((512, 512), BF16),
            pltpu.VMEM((512, 512), BF16),
            pltpu.VMEM((512, 512), BF16),
            pltpu.VMEM((512, 512), BF16),
            pltpu.VMEM((256, 256), BF16),
            pltpu.VMEM((256, 256), BF16),
            pltpu.VMEM((512, 512), BF16),
            pltpu.VMEM((512, 512), BF16),
            pltpu.VMEM((512, 512), BF16),
            pltpu.VMEM((512, 512), BF16),
            pltpu.VMEM((512, 512), F32),
            pltpu.SemaphoreType.DMA((6, 6)),
            pltpu.SemaphoreType.DMA((6, 6)),
            pltpu.SemaphoreType.DMA((3, 2)),
            pltpu.SemaphoreType.DMA((3,)),
        ],
        compiler_params=pltpu.CompilerParams(
            collective_id=0, has_side_effects=True, vmem_limit_bytes=53 * 2**20
        ),
        name="smooth_planes",
    )(model_gradient.reshape(params, 4, 2, 256, depth), filter_x, filter_y, filter_z, depth_scale)
    return result.reshape(params, xloc, yloc, depth)


def solution(mesh):
    return jax.shard_map(
        shards,
        mesh=mesh,
        in_specs=(P(None, "row", "col", None), P(), P(), P(), P()),
        out_specs=P(None, "row", "col", None),
        check_vma=False,
    )
```

time: 159 us -> 150 us (0.943)
  Pallas kernels: 156 us -> 147 us
    pallas_call x1, Pallas kernels: 156 us -> 147 us  [shards(): pl.pallas_call(kernel, out_shape=pltpu.VMEM((params, 4, 2, 256, depth), F...]
where the time goes in v3:
time: 150 us; the launch traced here: 149 us
  Pallas kernels  147 us (98%)
  local copies, waits for them, and re-layouts  2.71 us (2%)
    pallas_call x1, Pallas kernels, shards(): pl.pallas_call(kernel, out_shape=pltpu.VMEM((params, 4, 2, 256, depth), F...  147 us

profile of v3, /device:TPU:1, one launch (start us, length us, event | category | flops | bytes accessed | tf_op | source)
XLA Modules:
  0.0 149.4 jit_solution(4073410442986232850)
XLA Ops:
  0.0 146.7 %smooth_planes.1 = f32[3,4,2,256,256]{4,3,2,1,0:T(8,128)S(1)} custom-call(f32[3,4,2,256,256]{4,3,2,1,0:T(8,128)} %bitcast.3, f32[512,512]{1,0:T(8,128)} %fx_hbm.1, f32[512,512]{1,0:T(8,128)} %fy_hbm.1, f32[256,256]{1,0:T(8,128)} %fz_hbm.1, f32[3,256]{1,0:T(4,128)} %scale_ref.1), custom_call_target="tpu_custom_call" | custom-call | tf_op jit(solution)/shard_map/smooth_planes/pallas_call | solution.py:299
  146.7 2.7 %copy.7 = f32[3,64,32,256]{3,2,1,0:T(8,128)} copy(f32[3,64,32,256]{3,2,1,0:T(8,128)S(1)} %bitcast.2) | data formatting | bytes 12582912

commit v4 on v3

--- a/solution.py
+++ b/solution.py
@@ -64,16 +64,16 @@
     fz_copy = pltpu.make_async_copy(fz_hbm, wbuf.at[2, pl.ds(0, 256), pl.ds(0, 256)], w_sem.at[2])
     fx_copy = pltpu.make_async_copy(fx_hbm, wbuf.at[0], w_sem.at[0])
     fy_copy = pltpu.make_async_copy(fy_hbm, wbuf.at[1], w_sem.at[1])
+    fz_copy.start()
     load_in(0, 0).start()
-    fz_copy.start()
-    load_in(1, 0).start()
-    load_in(2, 0).start()
 
     barrier = pltpu.get_barrier_semaphore()
-    partners = [along(d, s, f) for d in "xyz" for s in (1, 2, 3) for f in (0, 1)]
+    partners = [along(d, s, f) for s in (2, 1, 3) for d in "xyz" for f in (0, 1)]
     partners.append(along("x", 0, 1))
     for at, k in partners:
         pl.semaphore_signal(barrier, inc=1, device_id=device(at, k), device_id_type=MESH)
+
+    load_in(1, 0).start()
 
     def transfers(c, stage, halves):
         order = ORDER[c % 3]
@@ -103,10 +103,11 @@
                     pairs = [
                         (b2.at[c, h * 8 + slot], b3.at[c, h, pl.ds(own * 128, 128)]) for h in halves
                     ]
-                for src, dst in pairs:
+                for i, (src, dst) in enumerate(pairs):
+                    line = 6 if stage == 5 and halves[i] == 1 else stage
                     found.append(
                         pltpu.make_async_remote_copy(
-                            src, dst, send_sem.at[c, stage], recv_sem.at[c, stage],
+                            src, dst, send_sem.at[c, stage], recv_sem.at[c, line],
                             device_id=device(at, k), device_id_type=MESH,
                         )
                     )
@@ -151,6 +152,8 @@
             return r1.at[c, pl.ds(0, 14)]
         if stage == 5:
             return b2.at[c, pl.ds(0, 14)]
+        if stage == 6:
+            return b2.at[c, pl.ds(0, 7)]
         return (r2, r3, b1, b2)[stage - 1].at[c, pl.ds(0, 12)]
 
     def arrived(c, stage):
@@ -162,42 +165,42 @@
         ref = whole(c, stage)
         pltpu.make_async_copy(ref, ref, send_sem.at[c, stage]).wait()
 
-    fz_copy.wait()
+    with jax.named_scope("fz"):
+        fz_copy.wait()
     fzh[...], fzl[...] = split(wbuf[2, 0:256, 0:256])
 
     def depth(p, j, h):
         fh, fl = fzh[j * 128 : j * 128 + 128], fzl[j * 128 : j * 128 + 128]
-        for it in range(4):
-            rows = [
-                out[p, b, h, m * 32 : m * 32 + 32] for m in (it * 2, it * 2 + 1) for b in range(4)
-            ]
-            high, low = split(jnp.concatenate(rows, axis=0))
-
-            def dot(a, b):
-                return lax.dot_general(
-                    a, b, (((1,), (1,)), ((), ())), preferred_element_type=F32
-                )
-
-            got = dot(fh, high) + dot(fl, high) + dot(fh, low)
-            for u in range(2):
-                s0[j * 3 + p, h, pl.ds(it * 2 + u, 128, stride=8)] = got[:, u * 128 : u * 128 + 128]
-
-    for h in range(2):
-        for p in range(3):
-            load_in(p, h).wait()
-            if h == 0:
-                load_in(p, 1).start()
-            with jax.named_scope(f"depth#c={p}#h={h}"):
-                depth(p, 0, h)
-            if h == 0 and p == 2:
-                fx_copy.start()
-                fy_copy.start()
-                with jax.named_scope("barrier"):
-                    pl.semaphore_wait(barrier, len(partners))
-                for c in range(3):
-                    send(c, 0, (0,))
-            if h == 1:
-                send(p, 0, (1,))
+        rows = [out[p, b, h, m * 32 : m * 32 + 32] for m in range(8) for b in range(4)]
+        high, low = split(jnp.concatenate(rows, axis=0))
+
+        def dot(a, b):
+            return lax.dot_general(a, b, (((1,), (1,)), ((), ())), preferred_element_type=F32)
+
+        got = dot(fh, high) + dot(fl, high) + dot(fh, low)
+        for m in range(8):
+            s0[j * 3 + p, h, pl.ds(m, 128, stride=8)] = got[:, m * 128 : m * 128 + 128]
+
+    for p in range(3):
+        load_in(p, 0).wait()
+        if p == 0:
+            load_in(2, 0).start()
+        else:
+            load_in(p - 1, 1).start()
+        with jax.named_scope(f"depth#c={p}#h=0"):
+            depth(p, 0, 0)
+    load_in(2, 1).start()
+    with jax.named_scope("barrier"):
+        pl.semaphore_wait(barrier, len(partners))
+    for c in range(3):
+        send(c, 0, (0,))
+    fx_copy.start()
+    fy_copy.start()
+    for p in range(3):
+        load_in(p, 1).wait()
+        with jax.named_scope(f"depth#c={p}#h=1"):
+            depth(p, 0, 1)
+        send(p, 0, (1,))
     for c in (3, 4, 5):
         for h in range(2):
             with jax.named_scope(f"depth#c={c}#h={h}"):
@@ -267,30 +270,50 @@
         with jax.named_scope(f"smooth#c={c}"):
             smooth(c)
         send(c, 3)
-    for stage in (4, 5):
-        for c in order:
-            arrived(c, stage - 1)
-            send(c, stage)
-
-    for c in range(6):
+    for c in order:
+        arrived(c, 3)
+        send(c, 4)
+    for c in order:
+        arrived(c, 4)
+        send(c, 5, (0,))
+        send(c, 5, (1,))
+
+    def finish(c, h):
         half, p = CHUNKS[c]
-        arrived(c, 5)
-
-        with jax.named_scope(f"final#c={c}"):
-
-            for h in range(2):
-                for m in range(8):
-                    turned = b3[c, h, pl.ds(m, 128, stride=8)].T
-                    turned = turned * scale_ref[p : p + 1, half * 128 : half * 128 + 128]
-                    for b in range(4):
-                        out[p, b, h, m * 32 : m * 32 + 32, half * 128 : half * 128 + 128] = turned[
-                            b * 32 : b * 32 + 32
-                        ]
-
+        cut = slice(half * 128, half * 128 + 128)
+        for m in range(8):
+            turned = b3[c, h, pl.ds(m, 128, stride=8)].T * scale_ref[p : p + 1, cut]
+            for b in range(4):
+                out[p, b, h, m * 32 : m * 32 + 32, cut] = turned[b * 32 : b * 32 + 32]
+
+    def arrived_last(c, h):
+        ref = whole(c, 6)
+        with jax.named_scope(f"last#c={c}#h={h}"):
+            pltpu.make_async_copy(ref, ref, recv_sem.at[c, 5 + h]).wait()
+
+    for c in order[:3]:
+        arrived_last(c, 0)
+        finish(c, 0)
+    for c in order[:3]:
+        arrived_last(c, 1)
+        finish(c, 1)
     with jax.named_scope("drain"):
         for c in range(6):
-            for stage in range(6):
+            for stage in range(5):
                 sent(c, stage)
+    for c in order[3:]:
+        arrived_last(c, 0)
+        finish(c, 0)
+    for c in order[:3]:
+        sent(c, 5)
+    for c in order[3:]:
+        arrived_last(c, 1)
+    with jax.named_scope("final"):
+        for c in order[3:]:
+            finish(c, 1)
+    with jax.named_scope("drain2"):
+        for c in order[3:]:
+            sent(c, 5)
 
 
 def shards(model_gradient, filter_x, filter_y, filter_z, depth_scale):
@@ -322,7 +345,7 @@
             pltpu.VMEM((512, 512), BF16),
             pltpu.VMEM((512, 512), F32),
             pltpu.SemaphoreType.DMA((6, 6)),
-            pltpu.SemaphoreType.DMA((6, 6)),
+            pltpu.SemaphoreType.DMA((6, 7)),
             pltpu.SemaphoreType.DMA((3, 2)),
             pltpu.SemaphoreType.DMA((3,)),
         ],

time: 150 us -> 150 us (level)
  no operation moved by 1% of the time
where the time goes in v4:
time: 150 us; the launch traced here: 149 us
  Pallas kernels  147 us (98%)
  local copies, waits for them, and re-layouts  2.71 us (2%)
    pallas_call x1, Pallas kernels, shards(): pl.pallas_call(kernel, out_shape=pltpu.VMEM((params, 4, 2, 256, depth), F...  147 us

profile of v4, /device:TPU:1, one launch (start us, length us, event | category | flops | bytes accessed | tf_op | source)
XLA Modules:
  0.0 149.4 jit_solution(18267485014357133816)
XLA Ops:
  0.0 146.6 %smooth_planes.1 = f32[3,4,2,256,256]{4,3,2,1,0:T(8,128)S(1)} custom-call(f32[3,4,2,256,256]{4,3,2,1,0:T(8,128)} %bitcast.3, f32[512,512]{1,0:T(8,128)} %fx_hbm.1, f32[512,512]{1,0:T(8,128)} %fy_hbm.1, f32[256,256]{1,0:T(8,128)} %fz_hbm.1, f32[3,256]{1,0:T(4,128)} %scale_ref.1), custom_call_target="tpu_custom_call" | custom-call | tf_op jit(solution)/shard_map/smooth_planes/pallas_call | solution.py:322
  146.7 2.7 %copy.7 = f32[3,64,32,256]{3,2,1,0:T(8,128)} copy(f32[3,64,32,256]{3,2,1,0:T(8,128)S(1)} %bitcast.2) | data formatting | bytes 12582912

commit v5 on v4

--- a/solution.py
+++ b/solution.py
@@ -316,6 +316,18 @@
             sent(c, 5)
 
 
+def write_out(held, out_hbm, sem):
+    copies = [
+        pltpu.make_async_copy(held.at[p, b], out_hbm.at[p, b], sem.at[p, b])
+        for p in range(held.shape[0])
+        for b in range(4)
+    ]
+    for copy in copies:
+        copy.start()
+    for copy in copies:
+        copy.wait()
+
+
 def shards(model_gradient, filter_x, filter_y, filter_z, depth_scale):
     params, xloc, yloc, depth = model_gradient.shape
     anywhere = pl.BlockSpec(memory_space=pl.ANY)
@@ -354,6 +366,16 @@
         ),
         name="smooth_planes",
     )(model_gradient.reshape(params, 4, 2, 256, depth), filter_x, filter_y, filter_z, depth_scale)
+    result = pltpu.with_memory_space_constraint(result, pltpu.VMEM)
+    result = pl.pallas_call(
+        write_out,
+        out_shape=jax.ShapeDtypeStruct((params, 4, 2, 256, depth), F32),
+        in_specs=[pl.BlockSpec(memory_space=pltpu.VMEM)],
+        out_specs=anywhere,
+        scratch_shapes=[pltpu.SemaphoreType.DMA((params, 4))],
+        compiler_params=pltpu.CompilerParams(vmem_limit_bytes=16 * 2**20),
+        name="write_out",
+    )(result)
     return result.reshape(params, xloc, yloc, depth)
 
 

time: 150 us -> 150 us (level)
  local copies, waits for them, and re-layouts: 2.71 us -> 0 us
  Pallas kernels: 147 us -> 149 us
    pallas_call x0 -> x1, Pallas kernels: none -> 2.75 us  [shards(): pl.pallas_call(write_out, out_shape=jax.ShapeDtypeStruct((params, 4, 2, 2...]
    unnamed x1 -> x0, local copies, waits for them, and re-layouts: 2.71 us -> none
where the time goes in v5:
time: 150 us
  Pallas kernels  149 us (99%)
    pallas_call x1, Pallas kernels, shards(): pl.pallas_call(kernel, out_shape=pltpu.VMEM((params, 4, 2, 256, depth), F...  147 us

profile of v5, /device:TPU:1, one launch (start us, length us, event | category | flops | bytes accessed | tf_op | source)
XLA Modules:
  0.0 149.6 jit_solution(7479453159330793816)
XLA Ops:
  0.0 146.6 %smooth_planes.1.held = f32[3,4,2,256,256]{4,3,2,1,0:T(8,128)S(1)} custom-call(f32[3,4,2,256,256]{4,3,2,1,0:T(8,128)} %bitcast.2, f32[512,512]{1,0:T(8,128)} %fx_hbm.1, f32[512,512]{1,0:T(8,128)} %fy_hbm.1, f32[256,256]{1,0:T(8,128)} %fz_hbm.1, f32[3,256]{1,0:T(4,128)} %scale_ref.1), custom_call_target="tpu_custom_call" | custom-call | tf_op jit(solution)/shard_map/smooth_planes/pallas_call | solution.py:334
  146.7 2.8 %write_out.1 = f32[3,4,2,256,256]{4,3,2,1,0:T(8,128)} custom-call(f32[3,4,2,256,256]{4,3,2,1,0:T(8,128)S(1)} %smooth_planes.1.held), custom_call_target="tpu_custom_call" | custom-call | tf_op jit(solution)/shard_map/write_out/pallas_call | solution.py:370
